TPU v7x, 8 devices: a whole 2x2x1 slice. The times are simulated.
8 devices in a mesh: sys: 1 (over z), col: 2 (over y), row: 4 (over x, core).
Axes of the slice: x: 2, y: 2, z: 1, core: 2. Of those that a mesh axis runs over, the one named last changes fastest.
Arguments:
- lower_tri: float32 [2, 64, 64, 4096], P('sys', 'row', None, 'col')
Outputs:
- output 1: float32 [2, 64, 64, 4096], P('sys', 'row', None, 'col')
- output 2: float32 [2, 4, 2, 64, 64], P('sys')
- output 3: float32 [2, 4, 64, 64, 64], P('sys', None, 'row')
- output 4: float32 [2, 4, 64, 64], P('sys')
All inputs are finite; a program needn't handle non-finite values.
Results may differ from a plain program's by a relative error of at most 0.001.
Values sent between devices are 32-bit elements.
A program may use at most 1 GiB of HBM per device.

v0:
```python
import jax
import jax.numpy as jnp
from jax import lax
from jax.sharding import PartitionSpec as P

PANELS = 4
MAX_PREC = lax.Precision.HIGHEST


def mat_prod(form, left_op, right_op):
    return jnp.einsum(form, left_op, right_op, precision=MAX_PREC, preferred_element_type=jnp.float32)


def global_index(n_loc, blk_size, n_procs, coord):
    position = jnp.arange(n_loc)
    return ((position // blk_size) * n_procs + coord) * blk_size + position % blk_size


def block_select(n_src, n_dst, src_procs, src_coord, dst_procs, dst_coord):
    src_glob = jnp.arange(n_src) * src_procs + src_coord
    dst_glob = jnp.arange(n_dst) * dst_procs + dst_coord
    return (dst_glob[:, None] == src_glob[None, :]).astype(jnp.float32)


def move_blocks(values, select, blk_size):
    n_mat, n_rows, n_width = values.shape
    blocks = values.reshape(n_mat, n_rows // blk_size, blk_size, n_width)
    moved_blk = mat_prod('da,xanw->xdnw', select, blocks)
    return moved_blk.reshape(n_mat, select.shape[0] * blk_size, n_width)


def householder_panel(panel_cols, row_g, trail_start):
    n_mat = panel_cols.shape[0]
    n_width = panel_cols.shape[2]
    col_ids = jnp.arange(n_width)

    def qr_step(col_idx, state_in):
        work_mat, refl_vecs, tau_vals = state_in
        x_col = lax.dynamic_index_in_dim(work_mat, col_idx, axis=2, keepdims=False)
        pivot = trail_start + col_idx
        at_piv = row_g == pivot
        below_piv = row_g > pivot
        piv_stats = jnp.stack([jnp.sum(jnp.where(at_piv, x_col, 0.0), axis=1), jnp.sum(jnp.where(below_piv, x_col * x_col, 0.0), axis=1)], axis=1)
        piv_stats = lax.psum(piv_stats, 'row')
        alpha_val = piv_stats[:, 0]
        sigma_val = piv_stats[:, 1]
        norm_val = jnp.sqrt(alpha_val * alpha_val + sigma_val)
        beta_val = jnp.where(alpha_val >= 0, -norm_val, norm_val)
        tau_val = (beta_val - alpha_val) / beta_val
        new_vec = jnp.where(below_piv, x_col / (alpha_val - beta_val)[:, None], jnp.where(at_piv, 1.0, 0.0))
        proj_row = lax.psum(mat_prod('xm,xmn->xn', new_vec, work_mat), 'row')
        proj_row = jnp.where(col_ids > col_idx, proj_row, 0.0)
        work_mat = work_mat - (tau_val[:, None] * new_vec)[:, :, None] * proj_row[:, None, :]
        new_col = jnp.where(at_piv, beta_val[:, None], jnp.where(below_piv, 0.0, x_col))
        is_col = col_ids == col_idx
        work_mat = jnp.where(is_col, new_col[:, :, None], work_mat)
        refl_vecs = jnp.where(is_col, new_vec[:, :, None], refl_vecs)
        tau_vals = jnp.where(is_col, tau_val[:, None], tau_vals)
        return work_mat, refl_vecs, tau_vals

    init_state = (panel_cols, jnp.zeros_like(panel_cols), jnp.zeros((n_mat, n_width), jnp.float32))
    return lax.fori_loop(0, n_width, qr_step, init_state)


def build_tri(tau_vals, gram_mat):
    n_mat, n_width = tau_vals.shape
    col_ids = jnp.arange(n_width)

    def tri_step(col_idx, t_factor):
        s_col = jnp.where(col_ids < col_idx, lax.dynamic_index_in_dim(gram_mat, col_idx, axis=2, keepdims=False), 0.0)
        tau_val = lax.dynamic_index_in_dim(tau_vals, col_idx, axis=1, keepdims=False)
        t_col = -tau_val[:, None] * mat_prod('xpq,xq->xp', t_factor, s_col)
        t_col = jnp.where(col_ids == col_idx, tau_val[:, None], t_col)
        return jnp.where(col_ids == col_idx, t_col[:, :, None], t_factor)

    return lax.fori_loop(0, n_width, tri_step, jnp.zeros((n_mat, n_width, n_width), jnp.float32))


def solution(mesh):
    n_prow = mesh.shape['row']
    n_pcol = mesh.shape['col']

    def per_device(lower_tri):
        n_mat, n_rblk, blk_size, n_cloc = lower_tri.shape
        n_rloc = n_rblk * blk_size
        n_cblk = n_cloc // blk_size
        my_row = lax.axis_index('row')
        my_col = lax.axis_index('col')
        row_g = global_index(n_rloc, blk_size, n_prow, my_row)
        col_g = global_index(n_cloc, blk_size, n_pcol, my_col)
        to_col = block_select(n_rblk, n_cblk, n_prow, my_row, n_pcol, my_col)
        to_row = to_col.T
        keep_low = row_g[:, None] >= col_g[None, :]
        strict = row_g[:, None] > col_g[None, :]
        low_mat = lower_tri.reshape(n_mat, n_rloc, n_cloc)
        band_list = []
        refl_list = []
        tfac_list = []
        for panel_idx in range(PANELS):
            trail_start = (panel_idx + 1) * blk_size
            col_off = (panel_idx // n_pcol) * blk_size
            col_slab = jnp.where(my_col == panel_idx % n_pcol, low_mat[:, :, col_off:col_off + blk_size], 0.0)
            col_slab = lax.psum(col_slab, 'col')
            in_trail = (row_g >= trail_start)[None, :, None]
            panel_cols = jnp.where(in_trail, col_slab, 0.0)
            rfac_mat, refl_vecs, tau_vals = householder_panel(panel_cols, row_g, trail_start)
            gram_mat = lax.psum(mat_prod('xmn,xmp->xnp', refl_vecs, refl_vecs), 'row')
            t_factor = build_tri(tau_vals, gram_mat)
            diag_off = (panel_idx // n_prow) * blk_size
            rfac_off = ((panel_idx + 1) // n_prow) * blk_size
            diag_part = jnp.where(my_row == panel_idx % n_prow, col_slab[:, diag_off:diag_off + blk_size, :], 0.0)
            rfac_part = jnp.where(my_row == (panel_idx + 1) % n_prow, rfac_mat[:, rfac_off:rfac_off + blk_size, :], 0.0)
            band_list.append(lax.psum(jnp.stack([diag_part, rfac_part], axis=1), 'row'))
            v_col = lax.psum(move_blocks(refl_vecs, to_col, blk_size), 'row')
            yt_col = lax.psum(mat_prod('xtc,xtn->xcn', low_mat, refl_vecs), 'row')
            l_strict = jnp.where(strict, low_mat, 0.0)
            y_part = mat_prod('xtc,xcn->xtn', l_strict, v_col) + move_blocks(yt_col, to_row, blk_size)
            y_row = jnp.where(in_trail, lax.psum(y_part, 'col'), 0.0)
            y_row = mat_prod('xtn,xnp->xtp', y_row, t_factor)
            vt_y = lax.psum(mat_prod('xtn,xtp->xnp', refl_vecs, y_row), 'row')
            corr_mat = mat_prod('xqn,xqp->xnp', t_factor, vt_y)
            w_row = y_row - 0.5 * mat_prod('xtn,xnp->xtp', refl_vecs, corr_mat)
            w_col = lax.psum(move_blocks(w_row, to_col, blk_size), 'row')
            left_op = jnp.concatenate([refl_vecs, w_row], axis=2)
            right_op = jnp.concatenate([w_col, v_col], axis=2)
            update = mat_prod('xtn,xcn->xtc', left_op, right_op)
            low_mat = low_mat - jnp.where(keep_low, update, 0.0)
            refl_list.append(refl_vecs.reshape(n_mat, n_rblk, blk_size, blk_size))
            tfac_list.append(t_factor)
        done_rows = PANELS * blk_size
        final_mat = jnp.where((row_g[:, None] >= done_rows) & (col_g[None, :] >= done_rows), low_mat, 0.0)
        return (final_mat.reshape(n_mat, n_rblk, blk_size, n_cloc), jnp.stack(band_list, axis=1), jnp.stack(refl_list, axis=1), jnp.stack(tfac_list, axis=1))

    spec_low = P('sys', 'row', None, 'col')
    return jax.shard_map(per_device, mesh=mesh, in_specs=(spec_low,), out_specs=(spec_low, P('sys'), P('sys', None, 'row', None, None), P('sys')), check_vma=False)
```

profile of v0, /device:TPU:0, one launch (start us, length us, event | category | flops | bytes accessed | tf_op | source)
XLA Modules:
  0.0 6755.0 jit_solution(2968600436812842467)
XLA Ops:
  9.7 38.3 all-reduce.22.cloned.1.call-done
  49.8 1199.6 %while.136 = (s32[]{:T(128)}, f32[2,1024,64]{1,0,2:T(2,128)S(1)}, f32[2,1024,64]{1,0,2:T(2,128)S(1)}, f32[2,64]{1,0:T(2,128)S(1)}, s32[]{:T(128)}, /*index=5*/s32[]{:T(128)}, s32[]{:T(128)}, s32[]{:T(128)}) while((s32[]{:T(128)}, f32[2,1024,64]{1,0,2:T(2,128)S(1)}, f32[2,1024,64]{1,0,2:T(2,128)S(1)}, ...), condition=%wide.region_6.7_spmd.clone.clone, body=%wide.region_1.6_spmd.clone.clone.sunk | while | flops 2290328 | bytes 2736768 | solution.py:62
  1292.3 63.5 all-reduce.52.cloned.1.call-done
  1378.1 29.0 while.137
  1451.9 44.4 all-reduce.26.cloned.1.call-done
  1496.4 25.4 select_subtract_fusion.2
  1524.2 34.4 all-reduce.28.cloned.1.call-done
  1562.6 1297.8 %while.138 = (s32[]{:T(128)}, f32[2,1024,64]{1,0,2:T(2,128)S(1)}, f32[2,1024,64]{1,0,2:T(2,128)}, f32[2,64]{1,0:T(2,128)S(1)}, s32[]{:T(128)}, /*index=5*/s32[]{:T(128)}, s32[]{:T(128)}, s32[]{:T(128)}) while((s32[]{:T(128)}, f32[2,1024,64]{1,0,2:T(2,128)S(1)}, f32[2,1024,64]{1,0,2:T(2,128)}, ...), condition=%wide.region_21.22_spmd.clone.clone, body=%wide.region_16.21_spmd.clone.clone.sunk | while | flops 2290328 | bytes 2736768 | solution.py:62
  2908.7 66.4 all-reduce.50.cloned.1.call-done
  2997.5 29.2 while.139
  3063.9 43.5 all-reduce.32.cloned.1.call-done
  3107.4 25.6 select_subtract_fusion.1
  3135.7 34.4 all-reduce.34.cloned.1.call-done
  3174.8 1538.6 %while.140 = (s32[]{:T(128)}, f32[2,1024,64]{1,0,2:T(2,128)}, f32[2,1024,64]{1,0,2:T(2,128)}, f32[2,64]{1,0:T(2,128)S(1)}, s32[]{:T(128)}, /*index=5*/s32[]{:T(128)}, s32[]{:T(128)}, s32[]{:T(128)}) while((s32[]{:T(128)}, f32[2,1024,64]{1,0,2:T(2,128)}, f32[2,1024,64]{1,0,2:T(2,128)}, f32[2,64]{1,0:T(2,128)S(1)}, ...), condition=%wide.region_36.37_spmd.clone.clone, body=%wide.region_31.36_spmd.clone.clone.sunk | while | flops 2290328 | bytes 2736768 | solution.py:62
  4761.6 66.4 all-reduce.48.cloned.1.call-done
  4850.3 29.2 while.141
  4916.8 43.5 all-reduce.38.cloned.1.call-done
  4960.3 25.8 select_subtract_fusion
  4992.2 31.0 all-reduce.40.cloned.1.call-done
  5027.2 1445.9 %while.142 = (s32[]{:T(128)}, f32[2,1024,64]{1,0,2:T(2,128)S(1)}, f32[2,1024,64]{1,0,2:T(2,128)}, f32[2,64]{1,0:T(2,128)}, s32[]{:T(128)}, /*index=5*/s32[]{:T(128)}, s32[]{:T(128)}, s32[]{:T(128)}) while((s32[]{:T(128)}, f32[2,1024,64]{1,0,2:T(2,128)S(1)}, f32[2,1024,64]{1,0,2:T(2,128)}, f32[2,64]{1,0:T(2,128)}, ...), condition=%wide.region_51.52_spmd.clone.clone, body=%wide.region_46.51_spmd.clone.clone.sunk | while | flops 2290328 | bytes 2741040 | solution.py:62
  6527.6 60.3 all-reduce.46.cloned.1.call-done
  6610.2 29.3 while.143
  6679.5 40.2 all-reduce.44.cloned.1.call-done
  6721.7 26.3 subtract_select_fusion.4
  (6645 shorter events, 6042.8 us)
Async XLA Ops:
  7.2 40.8 all-reduce.22.cloned.1.call-start
  9.5 1346.3 %all-reduce.52.cloned.1.call-start = ((), (), s32[]{:S(2)}) async-start(), calls=%async_computation.15 | async-start | bytes 8388608 | tf_op jit(solution)/shard_map/psum | solution.py:114
  9.6 4900.2 %copy-start.21 = (s32[32]{0:T(128)}, s32[32]{0:T(128)S(1)}, u32[]{:S(2)}) copy-start(s32[32]{0:T(128)S(1)} %multiply_add_fusion.1) | copy-start | bytes 388
  9.6 4900.2 %copy-start.23 = (s32[16]{0:T(128)}, s32[16]{0:T(128)S(1)}, u32[]{:S(2)}) copy-start(s32[16]{0:T(128)S(1)} %multiply_add_fusion) | copy-start | bytes 196
  1249.3 201.6 %copy-start.5 = (f32[2,1024,64]{1,0,2:T(2,128)}, f32[2,1024,64]{1,0,2:T(2,128)S(1)}, u32[]{:S(2)}) copy-start(f32[2,1024,64]{1,0,2:T(2,128)S(1)} %get-tuple-element.848) | copy-start | bytes 1572868
  1274.3 138.5 %all-reduce.24.cloned.1.call-start = ((), (), s32[]{:S(2)}) async-start(), calls=%async_computation.1 | async-start | bytes 2097152 | tf_op jit(solution)/shard_map/psum | solution.py:118
  1378.0 118.3 %all-reduce.26.cloned.1.call-start = ((), (), s32[]{:S(2)}) async-start(), calls=%async_computation.2 | async-start | bytes 4194304 | tf_op jit(solution)/shard_map/psum | solution.py:123
  1450.9 107.7 %all-reduce.28.cloned.1.call-start = ((), (), s32[]{:S(2)}) async-start(), calls=%async_computation.3 | async-start | bytes 2097152 | tf_op jit(solution)/shard_map/psum | solution.py:103
  1524.1 1451.1 %all-reduce.50.cloned.1.call-start = ((), (), s32[]{:S(2)}) async-start(), calls=%async_computation.14 | async-start | bytes 8388608 | tf_op jit(solution)/shard_map/psum | solution.py:114
  2893.6 138.7 %all-reduce.30.cloned.1.call-start = ((), (), s32[]{:S(2)}) async-start(), calls=%async_computation.4 | async-start | bytes 2097152 | tf_op jit(solution)/shard_map/psum | solution.py:118
  2997.4 110.0 %all-reduce.32.cloned.1.call-start = ((), (), s32[]{:S(2)}) async-start(), calls=%async_computation.5 | async-start | bytes 4194304 | tf_op jit(solution)/shard_map/psum | solution.py:123
  3061.8 108.3 %all-reduce.34.cloned.1.call-start = ((), (), s32[]{:S(2)}) async-start(), calls=%async_computation.6 | async-start | bytes 2097152 | tf_op jit(solution)/shard_map/psum | solution.py:103
  3135.6 1692.5 %all-reduce.48.cloned.1.call-start = ((), (), s32[]{:S(2)}) async-start(), calls=%async_computation.13 | async-start | bytes 8388608 | tf_op jit(solution)/shard_map/psum | solution.py:114
  4746.5 138.7 %all-reduce.36.cloned.1.call-start = ((), (), s32[]{:S(2)}) async-start(), calls=%async_computation.7 | async-start | bytes 2097152 | tf_op jit(solution)/shard_map/psum | solution.py:118
  4850.3 110.0 %all-reduce.38.cloned.1.call-start = ((), (), s32[]{:S(2)}) async-start(), calls=%async_computation.8 | async-start | bytes 4194304 | tf_op jit(solution)/shard_map/psum | solution.py:123
  4914.7 108.4 %all-reduce.40.cloned.1.call-start = ((), (), s32[]{:S(2)}) async-start(), calls=%async_computation.9 | async-start | bytes 2097152 | tf_op jit(solution)/shard_map/psum | solution.py:103
  4988.7 1599.2 %all-reduce.46.cloned.1.call-start = ((), (), s32[]{:S(2)}) async-start(), calls=%async_computation.12 | async-start | bytes 8388608 | tf_op jit(solution)/shard_map/psum | solution.py:114
  4988.8 38.4 copy-start.30
  6506.4 138.7 %all-reduce.42.cloned.1.call-start = ((), (), s32[]{:S(2)}) async-start(), calls=%async_computation.10 | async-start | bytes 2097152 | tf_op jit(solution)/shard_map/psum | solution.py:118
  6610.1 29.3 copy-start.3
  6610.1 35.0 copy-start.31
  6610.1 109.6 %all-reduce.44.cloned.1.call-start = ((), (), s32[]{:S(2)}) async-start(), calls=%async_computation.11 | async-start | bytes 5242880 | tf_op jit(solution)/shard_map/psum | solution.py:123
  6675.7 46.0 copy-start.19
  6679.5 42.2 copy-start
  (277 other events, 395.2 us)
Sparse Core Ops, SparseCore 0:
  10.8 37.0 all-reduce.21
  1274.4 81.3 all-reduce.51
  1378.2 34.5 all-reduce.23
  1451.0 45.2 all-reduce.25
  1524.2 34.3 all-reduce.27
  2893.8 81.3 all-reduce.49
  2997.5 34.7 all-reduce.29
  3061.9 45.3 all-reduce.31
  3135.7 34.3 all-reduce.33
  4746.6 81.3 all-reduce.47
  4850.4 34.7 all-reduce.35
  4914.9 45.3 all-reduce.37
  4988.8 34.3 all-reduce.39
  6506.5 81.3 all-reduce.45
  6610.3 34.7 all-reduce.41
  6665.7 53.9 all-reduce.43
where the time goes:
time: 6800 us; the launch traced here: 6750 us
  blocking collectives  4350 us (64%)
  other arithmetic  952 us (14%)
  waiting for transfers between devices  587 us (9%)
  matrix products  581 us (9%)
  local copies, waits for them, and re-layouts  238 us (4%)
    psum x256, blocking collectives, qr_step(): proj_row = lax.psum(mat_prod('xm,xmn->xn', new_vec, work_mat), 'row')  2790 us
    psum x256, blocking collectives, qr_step(): piv_stats = lax.psum(piv_stats, 'row')  1460 us
    dot_general x556, matrix products, mat_prod(): jnp.einsum(form, left_op, right_op, precision=MAX_PREC, preferred_element...  581 us
    select_n x256, other arithmetic, qr_step(): refl_vecs = jnp.where(is_col, new_vec[:, :, None], refl_vecs)  545 us
    psum x4, waiting for transfers between devices, per_device(): v_col = lax.psum(move_blocks(refl_vecs, to_col, blk_size), 'row')  257 us
    psum x4, waiting for transfers between devices, per_device(): w_col = lax.psum(move_blocks(w_row, to_col, blk_size), 'row')  172 us
    psum x4, waiting for transfers between devices, per_device(): col_slab = lax.psum(col_slab, 'col')  138 us

commit v1 on v0

v1 whole, which is shorter than its diff:
```python
import functools

import jax
import jax.numpy as jnp
from jax import lax
from jax.experimental import pallas as pl
from jax.experimental.pallas import tpu as pltpu
from jax.sharding import PartitionSpec as P

PANELS = 4
NB = 64
N = 4096
QTR = 1024
N_CH = N // 128
TR, TC = 256, 512
F32 = jnp.float32
BF16 = jnp.bfloat16
MESH = pl.DeviceIdType.MESH
VMEM_LIMIT = 60 * 1024 * 1024


def split3(a):
    hi = a.astype(BF16)
    rest = a - hi.astype(F32)
    mid = rest.astype(BF16)
    low = (rest - mid.astype(F32)).astype(BF16)
    return hi, mid, low


def bdot(a, b, ca=1, cb=0):
    return lax.dot_general(a, b, (((ca,), (cb,)), ((), ())), preferred_element_type=F32)


def fold_rows(x):
    n = x.shape[0] // 3
    return x[2 * n :] + x[n : 2 * n] + x[:n]


def mm(a, b, cb=0):
    lhs = jnp.concatenate(split3(a), axis=0)
    b1, b2, b3 = split3(b)
    return fold_rows(bdot(lhs, b3, 1, cb) + bdot(lhs, b2, 1, cb) + bdot(lhs, b1, 1, cb))


def gram(a_ref, b_ref, mask=None):
    acc = None
    for t in range(N // 512):
        sl = slice(t * 512, (t + 1) * 512)
        lhs = jnp.concatenate(split3(a_ref[:, sl]), axis=0)
        rhs = jnp.concatenate(split3(b_ref[:, sl]), axis=0)
        part = bdot(lhs, rhs, 1, 1)
        acc = part if acc is None else acc + part
    acc = fold_rows(acc)
    return acc[:, 128:192] + acc[:, 64:128] + acc[:, 0:64]


def bcast(v):
    return jnp.broadcast_to(v, (8, 128))


def qr_step(a_ref, xcur, xnext, stats, pc, pl0, gi, s, last_of_pair, accs):
    beta_ref, inv_ref, tau_ref = stats
    lane = lax.broadcasted_iota(jnp.int32, (8, 128), 1)
    sub = lax.broadcasted_iota(jnp.int32, (8, 1), 0)
    n_g = 8 - gi
    j = gi * 8 + s
    p = pl0 + j
    rows = [slice((gi + g) * 8, (gi + g + 1) * 8) for g in range(n_g)]
    dots = [jnp.sum(acc, axis=1, keepdims=True) for acc in accs]
    pvs = [jnp.sum(jnp.where(lane == p, a_ref[pc, r, :], 0.0), axis=1, keepdims=True) for r in rows]
    sigma = jnp.sum(jnp.where(sub == s, dots[0], 0.0), axis=0, keepdims=True)
    alpha = jnp.sum(jnp.where(sub == s, pvs[0], 0.0), axis=0, keepdims=True)
    sq = alpha * alpha + sigma
    inv_norm = lax.rsqrt(sq)
    norm = jnp.sqrt(sq)
    pos = alpha >= 0
    beta = jnp.where(pos, -norm, norm)
    ninvb = jnp.where(pos, inv_norm, -inv_norm)
    denom = alpha - beta
    inv_den = 1.0 / denom
    tau = denom * ninvb
    cs = [(pv + d * inv_den) * ninvb for pv, d in zip(pvs, dots)]
    cs[0] = jnp.where(sub > s, cs[0], 0.0)
    beta_ref[pl.ds(j, 1), :] = jnp.broadcast_to(beta, (1, 128))
    inv_ref[pl.ds(j, 1), :] = jnp.broadcast_to(inv_den, (1, 128))
    tau_ref[pl.ds(j, 1), :] = jnp.broadcast_to(tau, (1, 128))
    c_next = jnp.sum(jnp.where(sub == s + 1, cs[0], 0.0), axis=0, keepdims=True)
    if last_of_pair and n_g > 1:
        c_next = c_next + jnp.where(s == 7, cs[1][0:1], 0.0)
    jn = jnp.minimum(j + 1, NB - 1)
    c_next = bcast(c_next)
    den_b = bcast(denom)
    for ch in range(N_CH):
        xt = xcur[ch]
        if ch == pc:
            xt = jnp.where(lane == p, den_b, xt)
        xn = a_ref[ch, pl.ds(jn, 8, stride=0), :] - c_next * xt
        if ch == pc:
            xn = jnp.where(lane > p + 1, xn, 0.0)
        xnext[ch] = xn
    cs = [bcast(c) for c in cs]
    out = [jnp.zeros((8, 128), F32) for _ in range(n_g)]
    for ch in range(N_CH):
        xt = xcur[ch]
        if ch == pc:
            xt = jnp.where(lane == p, den_b, xt)
        xn = xnext[ch]
        for g in range(n_g):
            a = a_ref[ch, rows[g], :] - cs[g] * xt
            a_ref[ch, rows[g], :] = a
            out[g] = out[g] + a * xn
    return tuple(out)


def qr_panel(a_ref, x_refs, stats, pc, pl0):
    lane = lax.broadcasted_iota(jnp.int32, (8, 128), 1)
    accs = [jnp.zeros((8, 128), F32) for _ in range(8)]
    for ch in range(N_CH):
        x = bcast(a_ref[ch, 0:1, :])
        if ch == pc:
            x = jnp.where(lane > pl0, x, 0.0)
        x_refs[0][ch] = x
        for g in range(8):
            accs[g] = accs[g] + a_ref[ch, g * 8 : g * 8 + 8, :] * x
    accs = tuple(accs)
    for gi in range(8):

        def pair(h, accs, gi=gi):
            for par in range(2):
                accs = qr_step(a_ref, x_refs[par], x_refs[1 - par], stats, pc, pl0, gi, h * 2 + par, par == 1, accs)
            return accs

        accs = lax.fori_loop(0, 4, pair, accs)[1:]


def finish_panel(a_ref, stats, vt_ref, rt_ref, pc, pl0):
    beta_ref, inv_ref, tau_ref = stats
    lane = lax.broadcasted_iota(jnp.int32, (8, 128), 1)
    sub = lax.broadcasted_iota(jnp.int32, (8, 128), 0)
    for g in range(8):
        rows = slice(g * 8, g * 8 + 8)
        inv = inv_ref[rows, :]
        for ch in range(N_CH):
            sl = slice(ch * 128, (ch + 1) * 128)
            a = a_ref[ch, rows, :]
            v = a * inv
            if ch == pc:
                rel = lane - pl0 - (g * 8 + sub)
                rt_ref[rows, :] = jnp.where(rel < 0, a, jnp.where(rel == 0, beta_ref[rows, :], 0.0))
                v = jnp.where(rel > 0, v, jnp.where(rel == 0, 1.0, 0.0))
            vt_ref[rows, sl] = v


def build_tri(gram_mat, tau_col):
    row = lax.broadcasted_iota(jnp.int32, (NB, NB), 0)
    col = lax.broadcasted_iota(jnp.int32, (NB, NB), 1)
    t = jnp.where(row == col, tau_col, 0.0)
    for lg in range(6):
        rb = lax.shift_right_logical(row, lg)
        cb = lax.shift_right_logical(col, lg)
        u = jnp.where((cb == rb + 1) & (lax.rem(rb, 2) == 0), gram_mat, 0.0)
        t = t - mm(mm(t, u), t)
    return t


def panel_kernel(step, *refs):
    refs = list(refs)
    n_rem = PANELS - step
    if step > 0:
        vt_ref, yt_ref, t_ref, tt_ref = refs[:4]
        refs = refs[4:]
    if n_rem:
        pt_ref = refs.pop(0)
    if step > 0:
        wt_ref = refs.pop(0)
    if n_rem:
        d_ref, r_ref, vn_ref, tn_ref, ttn_ref = refs[:5]
        refs = refs[5:]
        if n_rem > 1:
            rem_ref = refs.pop(0)
    if n_rem:
        a_ref, xa, xb, beta_ref, inv_ref, tau_ref = refs
    lane64 = lax.broadcasted_iota(jnp.int32, (NB, 128), 1)
    row64 = lax.broadcasted_iota(jnp.int32, (NB, 128), 0)
    if step > 0:
        for g in range(step):
            sl = slice(g * QTR, g * QTR + 128)
            yt_ref[:, sl] = jnp.where(lane64 < NB, 0.0, yt_ref[:, sl])
        s_mat = gram(vt_ref, yt_ref)
        m_mat = mm(mm(tt_ref[...], s_mat, 1), t_ref[...])
        lhs = jnp.concatenate([tt_ref[...], -0.5 * m_mat], axis=1)
        for t in range(N // 512):
            sl = slice(t * 512, (t + 1) * 512)
            wt_ref[:, sl] = mm(lhs, jnp.concatenate([yt_ref[:, sl], vt_ref[:, sl]], axis=0))
    if not n_rem:
        return
    if step > 0:
        pieces = []
        for q in range(step, PANELS):
            sl = slice(q * QTR, q * QTR + 128)
            wc = wt_ref[:, sl].T[:NB]
            vc = vt_ref[:, sl].T[:NB]
            pieces.append(jnp.concatenate([wc, vc], axis=1))
        lhs = jnp.concatenate(pieces, axis=0)
        for t in range(N // 256):
            sl = slice(t * 256, (t + 1) * 256)
            upd = mm(lhs, jnp.concatenate([vt_ref[:, sl], wt_ref[:, sl]], axis=0))
            for h in range(2):
                a_ref[2 * t + h] = pt_ref[0, :, t * 256 + h * 128 : t * 256 + (h + 1) * 128] - upd[:NB, h * 128 : (h + 1) * 128]
            for q in range(1, n_rem):
                rem_ref[q - 1, :, sl] = pt_ref[q, :, sl] - upd[q * NB : (q + 1) * NB]
    else:
        for ch in range(N_CH):
            sl = slice(ch * 128, (ch + 1) * 128)
            a_ref[ch] = pt_ref[0, :, sl]
        for q in range(1, n_rem):
            rem_ref[q - 1] = pt_ref[q]
    d_ref[...] = jnp.where((lane64 >= row64) & (lane64 < NB), a_ref[step * 8], 0.0)
    for g in range(step + 1):
        a_ref[g * 8] = jnp.where(lane64 < NB, 0.0, a_ref[g * 8])
    pc = ((step + 1) % 4) * (QTR // 128)
    pl0 = NB * ((step + 1) // 4)
    stats = (beta_ref, inv_ref, tau_ref)
    qr_panel(a_ref, (xa, xb), stats, pc, pl0)
    finish_panel(a_ref, stats, vn_ref, r_ref, pc, pl0)
    t_new = build_tri(gram(vn_ref, vn_ref), tau_ref[:, :NB])
    tn_ref[...] = t_new
    ttn_ref[...] = jnp.concatenate([t_new, jnp.zeros((NB, NB), F32)], axis=1).T[:NB]


def panel_call(step, *args):
    n_rem = PANELS - step
    outs = []
    full = jax.ShapeDtypeStruct((NB, N), F32)
    small = jax.ShapeDtypeStruct((NB, NB), F32)
    wide = jax.ShapeDtypeStruct((NB, 128), F32)
    scratch = []
    if step > 0:
        outs.append(full)
    if n_rem:
        outs += [wide, wide, full, small, small]
        if n_rem > 1:
            outs.append(jax.ShapeDtypeStruct((n_rem - 1, NB, N), F32))
        scratch = [pltpu.VMEM((N_CH, NB, 128), F32), pltpu.VMEM((N_CH, 8, 128), F32), pltpu.VMEM((N_CH, 8, 128), F32)] + [pltpu.VMEM((NB, 128), F32)] * 3
    vspec = pl.BlockSpec(memory_space=pltpu.VMEM)
    return pl.pallas_call(
        functools.partial(panel_kernel, step),
        out_shape=outs,
        in_specs=[vspec] * len(args),
        out_specs=[vspec] * len(outs),
        scratch_shapes=scratch,
        compiler_params=pltpu.CompilerParams(vmem_limit_bytes=VMEM_LIMIT),
        name=f"panel{step}",
    )(*args)


def tile_kernel(update, products, final, *refs):
    refs = list(refs)
    l_ref = refs.pop(0)
    if products:
        va, vb = refs[:2]
        refs = refs[2:]
    if update:
        ua, ub, wa, wb = refs[:4]
        refs = refs[4:]
        lo_ref = refs.pop(0)
    if products:
        p1_ref, p2_ref = refs[:2]
        refs = refs[2:]
        vc3, vr3, acc1, acc2 = refs[:4]
        refs = refs[4:]
    if update:
        left6, right6 = refs
    mat = pl.program_id(0)
    ti = pl.program_id(1)
    tj = pl.program_id(2)
    my_row = lax.axis_index('row')
    my_col = lax.axis_index('col')
    mine = lax.rem(my_row, 2) == mat
    lane = lax.broadcasted_iota(jnp.int32, (NB, 128), 1)
    low_half = lane < NB

    def pick(a_ref, b_ref, base, ch):
        sl = pl.ds(pl.multiple_of(base * QTR + ch * 128, 128), 128)
        return jnp.where(mine, a_ref[:, sl], b_ref[:, sl])

    def col_chunks(a_ref, b_ref, u):
        qa = pick(a_ref, b_ref, my_col, u)
        qb = pick(a_ref, b_ref, my_col + 2, u)
        even = jnp.where(low_half, qa, pltpu.roll(qb, NB, 1))
        odd = jnp.where(low_half, pltpu.roll(qa, NB, 1), qb)
        return even, odd

    @pl.when((ti == 0) & (tj == 0))
    def _():
        if products:
            acc2[...] = jnp.zeros_like(acc2)
            vc3[192:256, :] = jnp.zeros((64, 2048), BF16)
            for u in range(8):
                for h, part in enumerate(col_chunks(va, vb, u)):
                    sl = slice((2 * u + h) * 128, (2 * u + h + 1) * 128)
                    for q, piece in enumerate(split3(part)):
                        vc3[q * NB : (q + 1) * NB, sl] = piece
                for q, piece in enumerate(split3(pick(va, vb, my_row, u))):
                    vr3[q * NB : (q + 1) * NB, u * 128 : (u + 1) * 128] = piece
        if update:
            for u in range(8):
                vcs = col_chunks(ua, ub, u)
                wcs = col_chunks(wa, wb, u)
                for h in range(2):
                    sl = slice((2 * u + h) * 128, (2 * u + h + 1) * 128)
                    r1, r2, r3 = split3(jnp.concatenate([wcs[h], vcs[h]], axis=0))
                    for q, piece in enumerate((r3, r2, r1, r2, r1, r1)):
                        right6[q * 128 : (q + 1) * 128, sl] = piece
                left = jnp.concatenate([pick(ua, ub, my_row, u), pick(wa, wb, my_row, u)], axis=0).T
                a1, a2, a3 = split3(left)
                for q, piece in enumerate((a1, a2, a3, a1, a2, a1)):
                    left6[u * 128 : (u + 1) * 128, q * 128 : (q + 1) * 128] = piece

    def run(diag):
        tile = l_ref[0]
        col_sl = pl.ds(pl.multiple_of(tj * TC, TC), TC)
        row_sl = pl.ds(pl.multiple_of(ti * TR, TR), TR)
        if diag or final:
            ri = lax.broadcasted_iota(jnp.int32, (TR, TC), 0) + ti * TR
            ci = lax.broadcasted_iota(jnp.int32, (TR, TC), 1) + tj * TC
            rg = (lax.shift_right_logical(ri, 6) * 4 + my_row) * NB + (ri & 63)
            cg = (lax.shift_right_logical(ci, 6) * 2 + my_col) * NB + (ci & 63)
        if update:
            upd = bdot(left6[row_sl, :], right6[:, col_sl])
            tile = tile - (jnp.where(rg >= cg, upd, 0.0) if diag else upd)
            if final:
                done = PANELS * NB
                lo_ref[0] = jnp.where((rg >= done) & (cg >= done), tile, 0.0)
            else:
                lo_ref[0] = tile
        if products:
            parts = split3(tile)
            vcols = vc3[:, col_sl]
            vrows = vr3[:, row_sl]
            p2 = None
            p1 = None
            for part in (parts[2], parts[1], parts[0]):
                q2 = bdot(vrows, part)
                p2 = q2 if p2 is None else p2 + q2
                q1 = bdot(jnp.where(rg == cg, jnp.zeros((), BF16), part) if diag else part, vcols, 1, 1)
                p1 = q1 if p1 is None else p1 + q1
            acc2[:, col_sl] += p2

            @pl.when(tj == 0)
            def _():
                acc1[...] = p1

            @pl.when(tj > 0)
            def _():
                acc1[...] += p1

            if diag:
                tot = (acc1[:, :128] + acc1[:, 128:]).T
                p1_ref[0, :, row_sl] = tot[NB:] + tot[:NB]

    @pl.when(tj < ti)
    def _():
        run(False)

    @pl.when(tj == ti)
    def _():
        run(True)

    if update and not final and len(update) == 1:

        @pl.when(tj > ti)
        def _():
            lo_ref[0] = jnp.zeros_like(lo_ref[0])

    if products:

        @pl.when((ti == 3) & (tj == 3))
        def _():
            for u in range(8):
                ev = fold_rows(acc2[:, 2 * u * 128 : (2 * u + 1) * 128])
                od = fold_rows(acc2[:, (2 * u + 1) * 128 : (2 * u + 2) * 128])
                sl = slice(u * 128, (u + 1) * 128)
                p2_ref[0, 0, :, sl] = jnp.where(low_half, ev, pltpu.roll(od, NB, 1))
                p2_ref[0, 1, :, sl] = jnp.where(low_half, pltpu.roll(ev, NB, 1), od)


def tile_call(low, v_pair, prev, in_place=False, final=False):
    products = v_pair is not None
    update = prev is not None
    lower_map = lambda m, i, j: (m, i, jnp.minimum(i, j))
    full_map = lambda m, i, j: (m, i, j)
    vspec = pl.BlockSpec(memory_space=pltpu.VMEM)
    args = [low]
    in_specs = [pl.BlockSpec((1, TR, TC), lower_map)]
    outs, out_specs, scratch = [], [], []
    if products:
        args += list(v_pair)
        in_specs += [vspec] * 2
    if update:
        args += list(prev)
        in_specs += [vspec] * 4
        outs.append(jax.ShapeDtypeStruct(low.shape, F32))
        out_specs.append(pl.BlockSpec((1, TR, TC), lower_map if in_place else full_map))
    if products:
        outs += [jax.ShapeDtypeStruct((2, NB, QTR), F32), jax.ShapeDtypeStruct((2, 2, NB, QTR), F32)]
        out_specs += [pl.BlockSpec((1, NB, QTR), lambda m, i, j: (m, 0, 0)), pl.BlockSpec((1, 2, NB, QTR), lambda m, i, j: (m, 0, 0, 0))]
        scratch += [pltpu.VMEM((256, 2048), BF16), pltpu.VMEM((192, QTR), BF16), pltpu.VMEM((TR, 256), F32), pltpu.VMEM((192, 2048), F32)]
    if update:
        scratch += [pltpu.VMEM((QTR, 768), BF16), pltpu.VMEM((768, 2048), BF16)]
    mode = () if not update else ((1, 1) if in_place else (1,))
    return pl.pallas_call(
        functools.partial(tile_kernel, mode, products, final),
        out_shape=outs,
        grid=(2, 4, 4),
        in_specs=in_specs,
        out_specs=out_specs,
        scratch_shapes=scratch,
        input_output_aliases={0: 0} if in_place else {},
        compiler_params=pltpu.CompilerParams(vmem_limit_bytes=VMEM_LIMIT, dimension_semantics=("arbitrary",) * 3),
        name="tiles",
    )(*args)


def barrier(neighbours):
    sem = pltpu.get_barrier_semaphore()
    for dev in neighbours:
        pl.semaphore_signal(sem, inc=1, device_id=dev, device_id_type=MESH)
    pl.semaphore_wait(sem, len(neighbours))


def remote(src, dst, send, recv, dev):
    return pltpu.make_async_remote_copy(src_ref=src, dst_ref=dst, send_sem=send, recv_sem=recv, device_id=dev, device_id_type=MESH)


def place():
    my_row = lax.axis_index('row')
    my_col = lax.axis_index('col')
    return lax.div(my_row, 2), lax.rem(my_row, 2), my_col


def device(x, core, y):
    return {'row': 2 * x + core, 'col': y}


def gather_kernel(slab_ref, pt_ref, send, recv):
    x, core, y = place()
    others = [(dx, dy, f) for dx in range(2) for dy in range(2) for f in range(2) if (dx, dy, f) != (0, 0, 0)]

    def flip(v, d):
        return 1 - v if d else v

    barrier([device(flip(x, dx), flip(core, f), flip(y, dy)) for dx, dy, f in others])
    lanes = pl.ds(pl.multiple_of((2 * x + core) * QTR, QTR), QTR)
    copies = []
    for blk in range(2):
        for idx, (dx, dy, f) in enumerate(others):
            to_core = flip(core, f)
            cp = remote(slab_ref.at[to_core, blk], pt_ref.at[2 * blk + y, :, lanes], send.at[blk, idx], recv.at[blk, idx], device(flip(x, dx), to_core, flip(y, dy)))
            cp.start()
            copies.append(cp)
    for blk in range(2):
        pt_ref[2 * blk + y, :, lanes] = slab_ref[core, blk]
    for cp in copies:
        cp.wait()


def gather_call(slab):
    vspec = pl.BlockSpec(memory_space=pltpu.VMEM)
    return pl.pallas_call(
        gather_kernel,
        out_shape=jax.ShapeDtypeStruct((PANELS, NB, N), F32),
        in_specs=[vspec],
        out_specs=vspec,
        scratch_shapes=[pltpu.SemaphoreType.DMA((2, 7)), pltpu.SemaphoreType.DMA((2, 7))],
        compiler_params=pltpu.CompilerParams(collective_id=0, has_side_effects=True, vmem_limit_bytes=VMEM_LIMIT),
        name="gather",
    )(slab)


def sum_kernel(p1, p2, yt, r_part, r_own, r_p1, r_p2, sbuf, qbuf, send, recv):
    x, core, y = place()
    partner = device(x, 1 - core, y)
    x_nbr = device(1 - x, core, y)
    y_nbr = device(x, core, 1 - y)
    y_cross = device(x, 1 - core, 1 - y)
    barrier([partner, x_nbr, y_nbr, y_cross])
    other = 1 - core
    c_part = remote(p2.at[other], r_part, send.at[0], recv.at[0], partner)
    c_part.start()
    c_y = remote(p1.at[core], r_p1, send.at[1], recv.at[1], y_nbr)
    c_yx = remote(p1.at[other], r_p1, send.at[2], recv.at[1], y_cross)
    c_own = remote(p1.at[other], r_own, send.at[1], recv.at[2], partner)

    @pl.when(core != y)
    def _():
        c_y.start()
        c_yx.start()

    @pl.when(core == y)
    def _():
        c_own.start()

    c_part.wait()
    sbuf[...] = p2[core, 1 - x] + r_part[1 - x]
    c_x = remote(sbuf, r_p2, send.at[3], recv.at[3], x_nbr)
    c_x.start()
    qbuf[...] = p2[core, x] + r_part[x]

    @pl.when(core == y)
    def _():
        c_own.wait_send()
        qbuf[...] += p1[core]

    @pl.when(core != y)
    def _():
        c_own.wait_recv()
        qbuf[...] += r_own[...]
        c_y.wait_send()
        c_yx.wait_send()

    c_y.wait_recv()
    qbuf[...] += r_p1[...]
    c_x.wait()
    qbuf[...] += r_p2[...]

    def lanes(xx, yy, half=None):
        start = (2 * xx + yy) * QTR
        if half is None:
            return pl.ds(pl.multiple_of(start, QTR), QTR)
        return pl.ds(pl.multiple_of(start + half * (QTR // 2), QTR // 2), QTR // 2)

    g_x = remote(qbuf, yt.at[:, lanes(x, y)], send.at[4], recv.at[4], x_nbr)
    g_y = remote(qbuf, yt.at[:, lanes(x, y)], send.at[5], recv.at[5], y_nbr)
    g_x.start()
    g_y.start()
    yt[:, lanes(x, y)] = qbuf[...]
    part_y = yt.at[:, lanes(x, 1 - y, 0)]
    f_x = remote(part_y, part_y, send.at[6], recv.at[6], x_nbr)
    part_x = yt.at[:, lanes(1 - x, y, 1)]
    f_y = remote(part_x, part_x, send.at[7], recv.at[7], y_nbr)
    g_y.wait_recv()
    f_x.start()
    g_x.wait_recv()
    f_y.start()
    g_x.wait_send()
    g_y.wait_send()
    f_x.wait()
    f_y.wait()


def sum_call(p1, p2):
    vspec = pl.BlockSpec(memory_space=pltpu.VMEM)
    qtr = pltpu.VMEM((NB, QTR), F32)
    return pl.pallas_call(
        sum_kernel,
        out_shape=jax.ShapeDtypeStruct((NB, N), F32),
        in_specs=[vspec] * 2,
        out_specs=vspec,
        scratch_shapes=[pltpu.VMEM((2, NB, QTR), F32), qtr, qtr, qtr, qtr, qtr, pltpu.SemaphoreType.DMA((8,)), pltpu.SemaphoreType.DMA((8,))],
        compiler_params=pltpu.CompilerParams(collective_id=1, has_side_effects=True, vmem_limit_bytes=VMEM_LIMIT),
        name="sums",
    )(p1, p2)


def swap_kernel(n, *refs):
    x, core, y = place()
    partner = device(x, 1 - core, y)
    barrier([partner])
    send, recv = refs[2 * n :]
    copies = [remote(refs[i], refs[n + i], send.at[i], recv.at[i], partner) for i in range(n)]
    for cp in copies:
        cp.start()
    for cp in copies:
        cp.wait()


def swap_call(ident, *arrays):
    n = len(arrays)
    vspec = pl.BlockSpec(memory_space=pltpu.VMEM)
    return pl.pallas_call(
        functools.partial(swap_kernel, n),
        out_shape=[jax.ShapeDtypeStruct(a.shape, F32) for a in arrays],
        in_specs=[vspec] * n,
        out_specs=[vspec] * n,
        scratch_shapes=[pltpu.SemaphoreType.DMA((n,)), pltpu.SemaphoreType.DMA((n,))],
        compiler_params=pltpu.CompilerParams(collective_id=ident, has_side_effects=True, vmem_limit_bytes=VMEM_LIMIT),
        name="swap",
    )(*arrays)


def solution(mesh):
    def per_device(lower_tri):
        n_mat, n_rblk, blk, n_cloc = lower_tri.shape
        n_rloc = n_rblk * blk
        my_row = lax.axis_index('row')
        core = lax.rem(my_row, 2)
        low = lower_tri.reshape(n_mat, n_rloc, n_cloc)
        slab = jnp.swapaxes(low[:, :, : 2 * NB], 1, 2).reshape(n_mat, 2, NB, n_rloc)
        pts = gather_call(slab)
        d_list, r_list, t_list, v_list = [], [], [], []
        prev = None
        wt = None
        for k in range(PANELS):
            if k == 0:
                d, r, vt, t, tt, pts = panel_call(0, pts)
                v_other, = swap_call(2, vt)
            else:
                out = panel_call(k, vt, yt, t, tt, pts)
                wt, d, r, vt_new, t, tt = out[:6]
                pts = out[6] if k < PANELS - 1 else None
                w_other, v_new_other = swap_call(3, wt, vt_new)
                prev = (vt, v_other, wt, w_other)
                vt, v_other = vt_new, v_new_other
            if k == 0:
                p1, p2 = tile_call(low, (vt, v_other), None)
            else:
                low, p1, p2 = tile_call(low, (vt, v_other), prev, in_place=k > 1)
            yt = sum_call(p1, p2)
            off = NB * ((k + 1) // 4)
            d_list.append(d[:, :NB].T)
            r_list.append(r[:, off : off + NB].T)
            t_list.append(t)
            pair = jnp.where(core == 0, jnp.stack([vt, v_other]), jnp.stack([v_other, vt]))
            mine = lax.dynamic_slice_in_dim(pair, my_row * QTR, QTR, axis=2)
            v_list.append(jnp.swapaxes(mine, 1, 2).reshape(n_mat, n_rblk, blk, blk))
        wt, = panel_call(PANELS, vt, yt, t, tt)
        packed = jnp.stack([jnp.stack(d_list), jnp.stack(r_list), jnp.stack(t_list)])
        packed = jnp.pad(packed.reshape(3 * PANELS * NB, NB), ((0, 0), (0, 128 - NB)))
        w_other, packed_other = swap_call(4, wt, packed)
        low, = tile_call(low, None, (vt, v_other, wt, w_other), in_place=True, final=True)
        both = jnp.where(core == 0, jnp.stack([packed, packed_other]), jnp.stack([packed_other, packed]))
        both = both[:, :, :NB].reshape(n_mat, 3, PANELS, NB, NB)
        band = jnp.stack([both[:, 0], both[:, 1]], axis=2)
        return low.reshape(lower_tri.shape), band, jnp.stack(v_list, axis=1), both[:, 2]

    spec_low = P('sys', 'row', None, 'col')
    return jax.shard_map(per_device, mesh=mesh, in_specs=(spec_low,), out_specs=(spec_low, P('sys'), P('sys', None, 'row', None, None), P('sys')), check_vma=False)
```

time: 6800 us -> 508 us (0.07)
  blocking collectives: 4350 us -> 0 us
  other arithmetic: 952 us -> 9.75 us
  waiting for transfers between devices: 587 us -> 0 us
  matrix products: 581 us -> 0 us
  Pallas kernels: 0 us -> 470 us
  local copies, waits for them, and re-layouts: 238 us -> 19.8 us
    psum x520 -> x0, blocking collectives: 4350 us -> none  [the longest x256 2790 us: qr_step(): proj_row = lax.psum(mat_prod('xm,xmn->xn', new_vec, work_mat), 'row')]
    select_n x2056 -> x1, other arithmetic: 721 us -> 0.05 us  [per_device(): jnp.where(core == 0, jnp.stack([packed, packed_other]), jnp.stack([packed...]
    psum x16 -> x0, waiting for transfers between devices: 587 us -> none  [the longest x4 257 us: per_device(): v_col = lax.psum(move_blocks(refl_vecs, to_col, blk_size), 'row')]
    dot_general x556 -> x0, matrix products: 581 us -> none  [mat_prod(): jnp.einsum(form, left_op, right_op, precision=MAX_PREC, preferred_element...]
    pallas_call x0 -> x20, Pallas kernels: none -> 470 us  [the longest x5 176 us: tile_call(): pl.pallas_call(functools.partial(tile_kernel, mode, products, final), out...]
    while x524 -> x0, local copies, waits for them, and re-layouts: 118 us -> none
    mul x512 -> x0, other arithmetic: 114 us -> none  [the longest x256 110 us: qr_step(): (tau_val[:, None] * new_vec)[:, :, None] * proj_row[:, None, :]]
    reduce_sum x256 -> x0, other arithmetic: 84.6 us -> none  [qr_step(): jnp.sum(jnp.where(at_piv, x_col, 0.0), axis=1)]
where the time goes in v1:
time: 508 us; the launch traced here: 500 us
  Pallas kernels  470 us (93%)
  local copies, waits for them, and re-layouts  19.8 us (4%)
  other arithmetic  9.75 us (2%)
    pallas_call x5, Pallas kernels, tile_call(): pl.pallas_call(functools.partial(tile_kernel, mode, products, final), out...  176 us
    pallas_call x5, Pallas kernels, panel_call(): pl.pallas_call(functools.partial(panel_kernel, step), out_shape=outs, in_...  110 us
    pallas_call x4, Pallas kernels, sum_call(): pl.pallas_call(sum_kernel, out_shape=jax.ShapeDtypeStruct((NB, N), F32),...  97.8 us
    pallas_call x1, Pallas kernels, gather_call(): pl.pallas_call(gather_kernel, out_shape=jax.ShapeDtypeStruct((PANELS, NB,...  53.6 us
    pallas_call x5, Pallas kernels, swap_call(): pl.pallas_call(functools.partial(swap_kernel, n), out_shape=[jax.ShapeDty...  32.2 us

profile of v1, /device:TPU:0, one launch (start us, length us, event | category | flops | bytes accessed | tf_op | source)
XLA Modules:
  0.0 500.5 jit_solution(9064249844349121652)
XLA Ops:
  3.2 53.6 %gather.1.refs_0_ = f32[4,64,4096]{2,1,0:T(8,128)} custom-call(f32[2,2,64,1024]{3,2,1,0:T(8,128)} %bitcast.96), custom_call_target="tpu_custom_call" | custom-call | tf_op jit(solution)/shard_map/gather/pallas_call | solution.py:470
  56.9 22.5 %panel0.1 = (f32[64,128]{1,0:T(8,128)}, f32[64,128]{1,0:T(8,128)}, f32[64,4096]{1,0:T(8,128)}, f32[64,64]{1,0:T(8,128)}, f32[64,64]{1,0:T(8,128)}, /*index=5*/f32[3,64,4096]{2,1,0:T(8,128)}) custom-call(f32[4,64,4096]{2,1,0:T(8,128)} %gather.1.refs_0_), custom_call_target="tpu_custom_call" | custom-call | tf_op jit(solution)/shard_map/panel0/pallas_call | solution.py:246
  81.1 5.2 %swap.5.refs_2_.refs_4_ = f32[64,4096]{1,0:T(8,128)} custom-call(f32[64,4096]{1,0:T(8,128)} %get-tuple-element.49.refs_0_.refs_1_.refs_3_), custom_call_target="tpu_custom_call" | custom-call | tf_op jit(solution)/shard_map/swap/pallas_call | solution.py:581
  86.3 27.0 %tiles.5 = (f32[2,64,1024]{2,1,0:T(8,128)}, f32[2,2,64,1024]{3,2,1,0:T(8,128)}) custom-call(f32[2,1024,2048]{2,1,0:T(8,128)} %bitcast.86, f32[64,4096]{1,0:T(8,128)} %get-tuple-element.49.refs_0_.refs_1_.refs_3_, f32[64,4096]{1,0:T(8,128)} %swap.5.refs_2_.refs_4_), custom_call_target="tpu_custom_call" | custom-call | tf_op jit(solution)/shard_map/tiles/pallas_call | solution.py:412
  113.3 25.1 %sums.4.refs_1_ = f32[64,4096]{1,0:T(8,128)} custom-call(f32[2,64,1024]{2,1,0:T(8,128)} %get-tuple-element.50.p1, f32[2,2,64,1024]{3,2,1,0:T(8,128)} %get-tuple-element.51.p2), custom_call_target="tpu_custom_call" | custom-call | tf_op jit(solution)/shard_map/sums/pallas_call | solution.py:555
  138.5 29.2 %panel1.1 = (f32[64,4096]{1,0:T(8,128)}, f32[64,128]{1,0:T(8,128)}, f32[64,128]{1,0:T(8,128)}, f32[64,4096]{1,0:T(8,128)}, f32[64,64]{1,0:T(8,128)}, /*index=5*/f32[64,64]{1,0:T(8,128)}, f32[2,64,4096]{2,1,0:T(8,128)}) custom-call(f32[64,4096]{1,0:T(8,128)} %get-tuple-element.49.refs_0_.refs_1_.refs_3_, f32[64,4096]{1,0:T(8,128)} %sums.4.refs_1_, ...), custom_call_target="tpu_custom_call" | custom-call | tf_op jit(solution)/shard_map/panel1/pallas_call | solution.py:246
  169.6 7.1 %swap.6 = (f32[64,4096]{1,0:T(8,128)}, f32[64,4096]{1,0:T(8,128)}) custom-call(f32[64,4096]{1,0:T(8,128)} %get-tuple-element.56.refs_0_.refs_5_, f32[64,4096]{1,0:T(8,128)} %get-tuple-element.55.refs_1_.refs_0_.refs_3_), custom_call_target="tpu_custom_call" | custom-call | tf_op jit(solution)/shard_map/swap/pallas_call | solution.py:581
  178.8 2.4 copy.41
  181.2 2.3 copy.40
  183.5 43.2 %tiles.6 = (f32[2,1024,2048]{2,1,0:T(8,128)}, f32[2,64,1024]{2,1,0:T(8,128)}, f32[2,2,64,1024]{3,2,1,0:T(8,128)}) custom-call(f32[2,1024,2048]{2,1,0:T(8,128)} %bitcast.87, f32[64,4096]{1,0:T(8,128)} %get-tuple-element.55.refs_1_.refs_0_.refs_3_, f32[64,4096]{1,0:T(8,128)} %get-tuple-element.57.refs_2_.refs_4_, ...), custom_call_target="tpu_custom_call" | custom-call | tf_op jit(solution)/shard_map/tiles/pallas_call | solution.py:412
  226.7 24.3 %sums.5.refs_1_ = f32[64,4096]{1,0:T(8,128)} custom-call(f32[2,64,1024]{2,1,0:T(8,128)} %get-tuple-element.60.p1, f32[2,2,64,1024]{3,2,1,0:T(8,128)} %get-tuple-element.61.p2), custom_call_target="tpu_custom_call" | custom-call | tf_op jit(solution)/shard_map/sums/pallas_call | solution.py:555
  250.9 27.3 %panel2.1 = (f32[64,4096]{1,0:T(8,128)}, f32[64,128]{1,0:T(8,128)}, f32[64,128]{1,0:T(8,128)}, f32[64,4096]{1,0:T(8,128)}, f32[64,64]{1,0:T(8,128)}, /*index=5*/f32[64,64]{1,0:T(8,128)}, f32[1,64,4096]{2,1,0:T(8,128)}) custom-call(f32[64,4096]{1,0:T(8,128)} %get-tuple-element.55.refs_1_.refs_0_.refs_3_, f32[64,4096]{1,0:T(8,128)} %sums.5.refs_1_, ...), custom_call_target="tpu_custom_call" | custom-call | tf_op jit(solution)/shard_map/panel2/pallas_call | solution.py:246
  279.9 7.1 %swap.7 = (f32[64,4096]{1,0:T(8,128)}, f32[64,4096]{1,0:T(8,128)}) custom-call(f32[64,4096]{1,0:T(8,128)} %get-tuple-element.66.refs_0_.refs_5_, f32[64,4096]{1,0:T(8,128)} %get-tuple-element.65.refs_1_.refs_0_.refs_3_), custom_call_target="tpu_custom_call" | custom-call | tf_op jit(solution)/shard_map/swap/pallas_call | solution.py:581
  287.0 39.9 %tiles.7 = (f32[2,1024,2048]{2,1,0:T(8,128)}, f32[2,64,1024]{2,1,0:T(8,128)}, f32[2,2,64,1024]{3,2,1,0:T(8,128)}) custom-call(f32[2,1024,2048]{2,1,0:T(8,128)} %get-tuple-element.59.refs_0_, f32[64,4096]{1,0:T(8,128)} %get-tuple-element.65.refs_1_.refs_0_.refs_3_, f32[64,4096]{1,0:T(8,128)} %get-tuple-element.67.refs_2_.refs_4_, ...), custom_call_target="tpu_custom_call", output_to_operand_aliasing={{0}: (0, {})} | custom-call | tf_op jit(solution)/shard_map/tiles/pallas_call | solution.py:412
  326.9 24.2 %sums.6.refs_1_ = f32[64,4096]{1,0:T(8,128)} custom-call(f32[2,64,1024]{2,1,0:T(8,128)} %get-tuple-element.70.p1, f32[2,2,64,1024]{3,2,1,0:T(8,128)} %get-tuple-element.71.p2), custom_call_target="tpu_custom_call" | custom-call | tf_op jit(solution)/shard_map/sums/pallas_call | solution.py:555
  351.1 25.2 %panel3.1 = (f32[64,4096]{1,0:T(8,128)}, f32[64,128]{1,0:T(8,128)}, f32[64,128]{1,0:T(8,128)}, f32[64,4096]{1,0:T(8,128)}, f32[64,64]{1,0:T(8,128)}, /*index=5*/f32[64,64]{1,0:T(8,128)}) custom-call(f32[64,4096]{1,0:T(8,128)} %get-tuple-element.65.refs_1_.refs_0_.refs_3_, f32[64,4096]{1,0:T(8,128)} %sums.6.refs_1_, f32[64,64]{1,0:T(8,128)} %get-tuple-element.72.refs_2_, ...), custom_call_target="tpu_custom_call" | custom-call | tf_op jit(solution)/shard_map/panel3/pallas_call | solution.py:246
  379.9 7.1 %swap.8 = (f32[64,4096]{1,0:T(8,128)}, f32[64,4096]{1,0:T(8,128)}) custom-call(f32[64,4096]{1,0:T(8,128)} %get-tuple-element.76.refs_0_.refs_5_, f32[64,4096]{1,0:T(8,128)} %get-tuple-element.75.refs_1_.refs_0_), custom_call_target="tpu_custom_call" | custom-call | tf_op jit(solution)/shard_map/swap/pallas_call | solution.py:581
  387.0 40.0 %tiles.8 = (f32[2,1024,2048]{2,1,0:T(8,128)}, f32[2,64,1024]{2,1,0:T(8,128)}, f32[2,2,64,1024]{3,2,1,0:T(8,128)}) custom-call(f32[2,1024,2048]{2,1,0:T(8,128)} %get-tuple-element.69.refs_0_, f32[64,4096]{1,0:T(8,128)} %get-tuple-element.75.refs_1_.refs_0_, f32[64,4096]{1,0:T(8,128)} %get-tuple-element.77.refs_2_, ...), custom_call_target="tpu_custom_call", output_to_operand_aliasing={{0}: (0, {})} | custom-call | tf_op jit(solution)/shard_map/tiles/pallas_call | solution.py:412
  430.7 2.3 copy.42
  433.1 3.8 pad_maximum_fusion
  436.9 24.2 %sums.7.refs_1_ = f32[64,4096]{1,0:T(8,128)} custom-call(f32[2,64,1024]{2,1,0:T(8,128)} %get-tuple-element.80.p1, f32[2,2,64,1024]{3,2,1,0:T(8,128)} %get-tuple-element.81.p2), custom_call_target="tpu_custom_call" | custom-call | tf_op jit(solution)/shard_map/sums/pallas_call | solution.py:555
  461.1 5.7 %panel4.1.refs_0_.refs_3_ = f32[64,4096]{1,0:T(8,128)} custom-call(f32[64,4096]{1,0:T(8,128)} %get-tuple-element.75.refs_1_.refs_0_, f32[64,4096]{1,0:T(8,128)} %sums.7.refs_1_, f32[64,64]{1,0:T(8,128)} %get-tuple-element.82.refs_2_, f32[64,64]{1,0:T(8,128)} %get-tuple-element.83.refs_3_), custom_call_target="tpu_custom_call" | custom-call | tf_op jit(solution)/shard_map/panel4/pallas_call | solution.py:246
  466.8 5.7 %swap.9 = (f32[64,4096]{1,0:T(8,128)}, f32[768,128]{1,0:T(8,128)}) custom-call(f32[64,4096]{1,0:T(8,128)} %panel4.1.refs_0_.refs_3_, f32[768,128]{1,0:T(8,128)} %get-tuple-element.98.refs_1_), custom_call_target="tpu_custom_call" | custom-call | tf_op jit(solution)/shard_map/swap/pallas_call | solution.py:581
  472.5 26.1 %tiles.9 = f32[2,1024,2048]{2,1,0:T(8,128)} custom-call(f32[2,1024,2048]{2,1,0:T(8,128)} %get-tuple-element.79.refs_0_, f32[64,4096]{1,0:T(8,128)} %get-tuple-element.75.refs_1_.refs_0_, f32[64,4096]{1,0:T(8,128)} %get-tuple-element.77.refs_2_, f32[64,4096]{1,0:T(8,128)} %panel4.1.refs_0_.refs_3_, ...), custom_call_target="tpu_custom_call", output_to_operand_aliasing={{}: (0, {})} | custom-call | tf_op jit(solution)/shard_map/tiles/pallas_call | solution.py:412
  (49 shorter events, 18.7 us)
Async XLA Ops:
  138.5 38.2 %copy-start.4 = (f32[64,4096]{1,0:T(8,128)S(1)}, f32[64,4096]{1,0:T(8,128)}, u32[]{:S(2)}) copy-start(f32[64,4096]{1,0:T(8,128)} %swap.5.refs_2_.refs_4_) | copy-start | bytes 3145732
  167.7 9.0 %copy-start.2 = (f32[64,4096]{1,0:T(8,128)S(1)}, f32[64,4096]{1,0:T(8,128)}, u32[]{:S(2)}) copy-start(f32[64,4096]{1,0:T(8,128)} %get-tuple-element.55.refs_1_.refs_0_.refs_3_) | copy-start | bytes 3145732
  167.7 9.0 %copy-start.3 = (f32[64,4096]{1,0:T(8,128)S(1)}, f32[64,4096]{1,0:T(8,128)}, u32[]{:S(2)}) copy-start(f32[64,4096]{1,0:T(8,128)} %get-tuple-element.49.refs_0_.refs_1_.refs_3_) | copy-start | bytes 3145732
  351.1 25.3 %copy-start.9 = (f32[64,64]{1,0:T(8,128)S(1)}, f32[64,64]{1,0:T(8,128)}, u32[]{:S(2)}) copy-start(f32[64,64]{1,0:T(8,128)} %get-tuple-element.62.refs_2_) | copy-start | bytes 49156
  351.1 25.3 %copy-start.10 = (f32[64,64]{1,0:T(8,128)S(1)}, f32[64,64]{1,0:T(8,128)}, u32[]{:S(2)}) copy-start(f32[64,64]{1,0:T(8,128)} %get-tuple-element.72.refs_2_) | copy-start | bytes 49156
  351.1 25.3 %copy-start.11 = (f32[64,64]{1,0:T(8,128)S(1)}, f32[64,64]{1,0:T(8,128)}, u32[]{:S(2)}) copy-start(f32[64,64]{1,0:T(8,128)} %get-tuple-element.52.refs_2_) | copy-start | bytes 49156
  387.0 40.0 %copy-start = (f32[64,4096]{1,0:T(8,128)S(1)}, f32[64,4096]{1,0:T(8,128)}, u32[]{:S(2)}) copy-start(f32[64,4096]{1,0:T(8,128)} %get-tuple-element.65.refs_1_.refs_0_.refs_3_) | copy-start | bytes 3145732
  387.0 40.0 %copy-start.1 = (f32[64,4096]{1,0:T(8,128)S(1)}, f32[64,4096]{1,0:T(8,128)}, u32[]{:S(2)}) copy-start(f32[64,4096]{1,0:T(8,128)} %get-tuple-element.75.refs_1_.refs_0_) | copy-start | bytes 3145732
  387.0 40.0 %copy-start.5 = (f32[64,4096]{1,0:T(8,128)S(1)}, f32[64,4096]{1,0:T(8,128)}, u32[]{:S(2)}) copy-start(f32[64,4096]{1,0:T(8,128)} %get-tuple-element.67.refs_2_.refs_4_) | copy-start | bytes 3145732
  429.2 3.9 copy-start.6
  429.2 3.9 copy-start.7
  472.5 26.1 %copy-start.8 = (f32[768,128]{1,0:T(8,128)S(1)}, f32[768,128]{1,0:T(8,128)}, u32[]{:S(2)}) copy-start(f32[768,128]{1,0:T(8,128)} %get-tuple-element.93) | copy-start | bytes 1179652
